TPU v7x, 128 devices: a whole 4x4x4 slice. The times are simulated.
128 devices in a mesh: tm: 8 (over z, core), row: 16 (over y, x).
Axes of the slice: x: 4, y: 4, z: 4, core: 2. Of those that a mesh axis runs over, the one named last changes fastest.
Arguments:
- visible: bfloat16 [8, 16, 16, 4, 1024], P('tm', 'row'), may hold values from -6 to 6
- slot_pos: int32 [8, 16, 16, 4], P('tm', 'row'), may hold values from -1 to 255, as said below
- window_shift: int32 [2, 2], replicated, may hold values from 0 to 3, as said below
- mask_token: bfloat16 [1024], replicated, may hold values from -6 to 6
- w_qkv: bfloat16 [1024, 3072], replicated, may hold values from -6.25 to 6.25
- w_out: bfloat16 [1024, 1024], replicated, may hold values from -0.1875 to 0.1875
- w_head: bfloat16 [1024, 1536], replicated, may hold values from -0.1875 to 0.1875
- pixels: bfloat16 [32, 64, 16, 1536], P('tm', 'row'), may hold values from 0 to 1
Outputs:
- d_visible: bfloat16 [8, 16, 16, 4, 1024], P('tm', 'row')
- d_mask_token: float32 [1024], replicated
Inputs may be any that keep to these rules, and one draw needn't show every extreme that they name: Each live entry slot_pos[i, s, d, c] is a token index of decoder shard (i, d) in frame, row, column order; the live entries aimed at one shard (i, d) are distinct; every slot slot_pos[i, s, s, c] is live, so each shard receives all 4 slots from the packed shard of its own band; other slots are live or -1 at rates that differ from packed shard to packed shard. window_shift[0, g] lies in 0 to 1 and window_shift[1, g] in 0 to 3; some block of columns has row offset 4 - 1 and some block has frame offset 0.
All inputs are finite; a program needn't handle non-finite values.
Results may differ from a plain program's by a relative error of at most 0.014.
Values may be sent and summed in bfloat16 or wider, within the bound.
No kernel may reach another device: no remote copies, remote signals or barrier semaphores. Data moves between devices by JAX's collectives and lax.ppermute only.
A program may use at most 128 MiB of HBM per device.

v0:
```python
import functools
import math

import jax
import jax.numpy as jnp
from jax import lax
from jax.experimental import pallas as pl
from jax.experimental.pallas import tpu as pltpu
from jax.sharding import Mesh
from jax.sharding import PartitionSpec as P

WT = 2
WH = 4
WW = 8
D = 1024
PIX = 1536
GROUP = PIX // 3
TOK = 256
HALF = TOK // 2
WIN = WT * WH * WW
PAIRS = D // 128
SLOTS = 128
TM = ("tm_0", "tm_1")
ROW = ("row_0", "row_1")
ALL = TM + ROW
BF = jnp.bfloat16
F32 = jnp.float32
NT_DIMS = (((1,), (1,)), ((), ()))
TN_DIMS = (((0,), (0,)), ((), ()))
NN_DIMS = (((1,), (0,)), ((), ()))
VMEM = pltpu.MemorySpace.VMEM
SMEM = pltpu.MemorySpace.SMEM
HBM = pltpu.MemorySpace.HBM


def dot(a, b, dims):
    return lax.dot_general(a, b, dims, preferred_element_type=F32)


def lane_mean(values):
    return jnp.sum(values, axis=-1, keepdims=True) * (1.0 / values.shape[-1])


def normalise(values):
    center = values - lane_mean(values)
    scale = lax.rsqrt(lane_mean(center * center) + 1e-05)
    return center * scale, scale


def normalise_back(cotangent, normed, scale):
    return scale * (cotangent - lane_mean(cotangent) - normed * lane_mean(cotangent * normed))


def two_heads(rows):
    first = lax.broadcasted_iota(jnp.int32, rows.shape, 1) < 64
    zero = jnp.zeros_like(rows)
    return jnp.concatenate([jnp.where(first, rows, zero), jnp.where(first, zero, rows)], axis=0)


def own_head(rows):
    first = lax.broadcasted_iota(jnp.int32, (WIN, 128), 1) < 64
    return jnp.where(first, rows[:WIN], rows[WIN:])


def slot_one_hot(shift_ref, rows_ref, behind, frame_pair):
    place = rows_ref[:, D : D + 128].astype(F32).astype(jnp.int32)
    frame = place >> 6
    row = (place >> 4) & 3
    column = place & 15
    group = column >> 3
    slot = lax.broadcasted_iota(jnp.int32, (SLOTS, 128), 0) & 7
    lane = lax.broadcasted_iota(jnp.int32, (SLOTS, 128), 1)
    frame = frame + jnp.where(group == 0, shift_ref[0:1], shift_ref[1:2]) - 4 * behind
    row = row + jnp.where(group == 0, shift_ref[2:3], shift_ref[3:4]) + jnp.where(slot >= 4, 4, 0)
    inside = (place >= 0) & ((frame >> 1) == frame_pair) & (row >= 0) & (row < 4)
    token = group * 64 + ((frame & 1) * 32) + row * 8 + (column & 7)
    token = jnp.where(inside, token, -1)
    return jnp.where(token == lane, 1.0, 0.0).astype(BF)


def embed(frame_pair, mask_ref, frames_ref, rows_ref, columns_ref, chosen_ref, seen_ref, embedded_ref, normed_ref):
    mask = mask_ref[...].astype(F32)
    mask = jnp.concatenate([mask[at : at + 1] for at in range(8)], axis=1)
    for block in range(HALF // 16):
        group, half = divmod(block, 4)
        at_frame = group * 4 + frame_pair * 2 + half // 2
        rows = slice(block * 16, block * 16 + 16)
        start = jnp.where(jnp.concatenate([seen_ref[rows]] * 8, axis=1) > 0, chosen_ref[rows], mask)
        position = []
        for at in range(2):
            at_row = group * 4 + (half % 2) * 2 + at
            position.append(
                jnp.concatenate(
                    [
                        jnp.broadcast_to(frames_ref[at_frame : at_frame + 1], (8, 256)),
                        jnp.broadcast_to(rows_ref[at_row : at_row + 1], (8, 384)),
                        columns_ref[group * 8 : group * 8 + 8],
                    ],
                    axis=1,
                )
            )
        embedded = (start + jnp.concatenate(position, axis=0)).astype(BF)
        embedded_ref[rows] = embedded
        normed_ref[rows] = normalise(embedded.astype(F32))[0].astype(BF)


def project(at, normed_ref, w_qkv_ref, qkv_ref):
    for part in range(2):
        cols = slice(at * D + part * 512, at * D + part * 512 + 512)
        qkv_ref[:, cols] = dot(normed_ref[...], w_qkv_ref[:, cols], NN_DIMS).astype(BF)


def attend(qkv_ref, probs_ref, heads_ref):
    for window in range(HALF // WIN):
        rows = slice(window * WIN, window * WIN + WIN)
        scores = []
        for pair in range(PAIRS):
            q = qkv_ref[rows, pair * 128 : pair * 128 + 128]
            k = qkv_ref[rows, D + pair * 128 : D + pair * 128 + 128]
            scores.append(dot(k, two_heads(q), NT_DIMS) * 0.125)
        probs = []
        for pair in range(PAIRS):
            weights = jnp.exp(scores[pair] - jnp.max(scores[pair], axis=0, keepdims=True))
            probs.append((weights * (1.0 / jnp.sum(weights, axis=0, keepdims=True))).astype(BF))
            probs_ref[window, pair] = probs[pair]
        for pair in range(PAIRS):
            v = qkv_ref[rows, 2 * D + pair * 128 : 2 * D + pair * 128 + 128]
            heads_ref[rows, pair * 128 : pair * 128 + 128] = own_head(dot(probs[pair], v, TN_DIMS)).astype(BF)


def early_kernel(
    shift_ref, own_ref, mask_ref, frames_ref, rows_ref, columns_ref, w_qkv_hbm, w_out_hbm, w_head_hbm,
    embedded_ref, qkv_ref, probs_ref, seen_ref, one_hot_ref, heads_ref, w_qkv_ref, w_out_ref, w_head_ref,
    chosen_ref, normed_ref, sems,
):
    copies = [
        pltpu.make_async_copy(
            w_qkv_hbm.at[:, pl.ds(at * D, D)], w_qkv_ref.at[:, pl.ds(at * D, D)], sems.at[at]
        )
        for at in range(3)
    ]
    copies.append(pltpu.make_async_copy(w_out_hbm, w_out_ref, sems.at[3]))
    copies.append(pltpu.make_async_copy(w_head_hbm, w_head_ref, sems.at[4]))
    for copy in copies:
        copy.start()
    one_hot_ref[...] = slot_one_hot(shift_ref, own_ref, 0, 1)
    chosen_ref[...] = dot(one_hot_ref[...], own_ref[:, :D], TN_DIMS)
    seen_ref[...] = dot(one_hot_ref[...], jnp.ones((SLOTS, 128), BF), TN_DIMS)
    embed(1, mask_ref, frames_ref, rows_ref, columns_ref, chosen_ref, seen_ref, embedded_ref, normed_ref)
    for at in range(3):
        copies[at].wait()
        project(at, normed_ref, w_qkv_ref, qkv_ref)
    attend(qkv_ref, probs_ref, heads_ref)
    copies[3].wait()
    copies[4].wait()


def late_kernel(
    shift_ref, own_ref, behind_ref, mask_ref, frames_ref, rows_ref, columns_ref, embedded_1_ref, heads_1_ref,
    w_qkv_ref, w_out_ref, w_head_ref,
    embedded_ref, qkv_ref, probs_ref, seen_ref, one_hot_ref, head_normed_ref, scale_ref, predicted_ref,
    chosen_ref, normed_ref, heads_ref, residual_ref, narrow_ref,
):
    one_hot_ref[:SLOTS] = slot_one_hot(shift_ref, own_ref, 0, 0)
    one_hot_ref[SLOTS:] = slot_one_hot(shift_ref, behind_ref, 1, 0)
    own_hot = one_hot_ref[:SLOTS]
    behind_hot = one_hot_ref[SLOTS:]
    chosen_ref[...] = dot(own_hot, own_ref[:, :D], TN_DIMS) + dot(behind_hot, behind_ref[:, :D], TN_DIMS)
    seen_ref[...] = dot(one_hot_ref[...], jnp.ones((2 * SLOTS, 128), BF), TN_DIMS)
    embed(0, mask_ref, frames_ref, rows_ref, columns_ref, chosen_ref, seen_ref, embedded_ref, normed_ref)
    for at in range(3):
        project(at, normed_ref, w_qkv_ref, qkv_ref)
    heads_ref[HALF:] = heads_1_ref[...]
    attend(qkv_ref, probs_ref, heads_ref)
    for part in range(2):
        cols = slice(part * 512, part * 512 + 512)
        attn = dot(heads_ref[...], w_out_ref[:, cols], NN_DIMS).astype(BF).astype(F32)
        residual_ref[:HALF, cols] = embedded_ref[:, cols].astype(F32) + attn[:HALF]
        residual_ref[HALF:, cols] = embedded_1_ref[:, cols].astype(F32) + attn[HALF:]
    for block in range(TOK // 16):
        rows = slice(block * 16, block * 16 + 16)
        normed, scale = normalise(residual_ref[rows])
        head_normed_ref[rows] = normed
        scale_ref[rows] = jnp.broadcast_to(scale, (16, 128))
        narrow_ref[rows] = normed.astype(BF)
    for part in range(3):
        cols = slice(part * GROUP, part * GROUP + GROUP)
        predicted_ref[:, cols] = dot(narrow_ref[...], w_head_ref[:, cols], NN_DIMS)


def backward_kernel(
    shift_ref, embedded_0_ref, qkv_0_ref, probs_0_ref, seen_0_ref, one_hot_0_ref,
    embedded_1_ref, qkv_1_ref, probs_1_ref, seen_1_ref, one_hot_1_ref,
    normed_ref, scale_ref, predicted_ref, w_qkv_ref, w_out_ref, w_head_ref,
    own_target, row_target, last_row_target, time_target, corner_target,
    own_picked_ref, behind_rows_ref, total_ref,
    target_ref, error_ref, narrow_ref, wide_ref, stream_ref, dqkv_ref,
):
    embedded_refs = (embedded_0_ref, embedded_1_ref)
    qkv_refs = (qkv_0_ref, qkv_1_ref)
    probs_refs = (probs_0_ref, probs_1_ref)
    seen_refs = (seen_0_ref, seen_1_ref)
    target_ref[1:, :4] = own_target[...]
    target_ref[:1, :4] = time_target[...]
    for frame in range(5):
        halo_ref, at_frame = (
            (corner_target, 0) if frame == 0 else (last_row_target, 0) if frame == 4 else (row_target, frame - 1)
        )
        target_ref[frame, 4] = halo_ref[at_frame, 0]
        halves = halo_ref[at_frame, 1].astype(F32)
        for at in range(2):
            half = halves[at * 8 : at * 8 + 8]
            target_ref[frame, 5 + at] = jnp.concatenate([half, half], axis=0).astype(BF)

    for block in range(TOK // 16):
        frame_pair, rest = divmod(block, 8)
        group, half = divmod(rest, 4)
        rows = slice(block * 16, block * 16 + 16)
        local = slice(rest * 16, rest * 16 + 16)
        masked = 1.0 - jnp.concatenate([seen_refs[frame_pair][local]] * 12, axis=1)
        target = jnp.concatenate(
            [
                target_ref[
                    frame_pair * 2 + half // 2 - shift_ref[0, group] + 1,
                    (half % 2) * 2 + at + ((4 - shift_ref[1, group]) & 3),
                    group * 8 : group * 8 + 8,
                ].astype(F32)
                for at in range(2)
            ],
            axis=0,
        )
        error_ref[rows] = (masked * (predicted_ref[rows] - target)).astype(BF)

    for part in range(2):
        cols = slice(part * 512, part * 512 + 512)
        wide_ref[:, cols] = dot(error_ref[...], w_head_ref[cols, :], NT_DIMS)

    for block in range(TOK // 16):
        rows = slice(block * 16, block * 16 + 16)
        scale = jnp.concatenate([scale_ref[rows]] * 8, axis=1)
        cotangent = wide_ref[rows].astype(BF).astype(F32)
        grad = normalise_back(cotangent, normed_ref[rows], scale)
        stream_ref[rows] = grad
        narrow_ref[rows] = grad.astype(BF)

    narrow_ref[...] = dot(narrow_ref[...], w_out_ref[...], NT_DIMS).astype(BF)

    for window in range(TOK // WIN):
        rows = slice(window * WIN, window * WIN + WIN)
        frame_pair, group = divmod(window, 2)
        local = slice(group * WIN, group * WIN + WIN)
        qkv_ref = qkv_refs[frame_pair]
        probs_ref = probs_refs[frame_pair]
        cols = [[slice(at * D + pair * 128, at * D + pair * 128 + 128) for at in range(3)] for pair in range(PAIRS)]
        d_probs = []
        out_heads = []
        for pair in range(PAIRS):
            out_heads.append(two_heads(narrow_ref[rows, cols[pair][0]]))
            d_probs.append(dot(qkv_ref[local, cols[pair][2]], out_heads[pair], NT_DIMS))
        for pair in range(PAIRS):
            dqkv_ref[rows, cols[pair][2]] = dot(probs_ref[group, pair], out_heads[pair], NN_DIMS).astype(BF)
        d_scores = []
        for pair in range(PAIRS):
            probs = probs_ref[group, pair].astype(F32)
            cotangent = d_probs[pair].astype(BF).astype(F32)
            mean = jnp.sum(cotangent * probs, axis=0, keepdims=True)
            d_scores.append((probs * (cotangent - mean) * 0.125).astype(BF))
        for pair in range(PAIRS):
            q_heads = two_heads(qkv_ref[local, cols[pair][0]])
            dqkv_ref[rows, cols[pair][1]] = dot(d_scores[pair], q_heads, NN_DIMS).astype(BF)
        for pair in range(PAIRS):
            d_q = own_head(dot(d_scores[pair], qkv_ref[local, cols[pair][1]], TN_DIMS))
            dqkv_ref[rows, cols[pair][0]] = d_q.astype(BF)

    for part in range(2):
        cols = slice(part * 512, part * 512 + 512)
        wide_ref[:, cols] = dot(dqkv_ref[...], w_qkv_ref[cols, :], NT_DIMS)

    total = jnp.zeros((8, D), F32)
    for block in range(TOK // 16):
        frame_pair, rest = divmod(block, 8)
        rows = slice(block * 16, block * 16 + 16)
        local = slice(rest * 16, rest * 16 + 16)
        normed, scale = normalise(embedded_refs[frame_pair][local].astype(F32))
        cotangent = wide_ref[rows].astype(BF).astype(F32)
        grad = stream_ref[rows] + normalise_back(cotangent, normed, scale)
        narrow_ref[rows] = grad.astype(BF)
        part = (1.0 - jnp.concatenate([seen_refs[frame_pair][local]] * 8, axis=1)) * grad
        total = total + part[:8] + part[8:]
    total = jnp.sum(total, axis=0, keepdims=True)
    total_ref[...] = jnp.concatenate([total[:, at * 128 : at * 128 + 128] for at in range(8)], axis=0)
    behind_rows_ref[...] = jnp.where(
        shift_ref[0, 1] == 1, narrow_ref[WIN : WIN + 32].astype(F32), narrow_ref[:32].astype(F32)
    ).astype(BF)
    own_picked = dot(one_hot_0_ref[:SLOTS], narrow_ref[:HALF], NN_DIMS)
    own_picked_ref[...] = (own_picked + dot(one_hot_1_ref[...], narrow_ref[HALF:], NN_DIMS)).astype(BF)


def give_kernel(
    shift_ref, own_ref, picked_ref, next_ref, total_ref, turned_1_ref, turned_2_ref, turned_3_ref, sent_ref
):
    place = own_ref[:, D : D + 128].astype(F32).astype(jnp.int32)
    row = (place >> 4) & 3
    column = place & 15
    slot = lax.broadcasted_iota(jnp.int32, (SLOTS, 128), 0) & 7
    lane = lax.broadcasted_iota(jnp.int32, (SLOTS, 128), 1)
    late = jnp.where(column < 8, shift_ref[0:1], shift_ref[1:2])
    row = row + jnp.where(column < 8, shift_ref[2:3], shift_ref[3:4]) + jnp.where(slot >= 4, 4, 0)
    inside = (place >= 192) & (late == 1) & (row >= 0) & (row < 4)
    token = jnp.where(inside, row * 8 + (column & 7), -1)
    one_hot = jnp.where(token == lane, 1.0, 0.0).astype(BF)
    rows = jnp.concatenate([next_ref[...], jnp.zeros((SLOTS - 32, D), BF)], axis=0)
    picked = picked_ref[...].astype(F32) + dot(one_hot, rows, NN_DIMS)
    sent_ref[:, :, :D] = picked.reshape(16, 8, D).astype(BF)
    total = (total_ref[...] + turned_2_ref[...]) + (turned_1_ref[...] + turned_3_ref[...])
    high = total.astype(BF)
    low = (total - high.astype(F32)).astype(BF)
    for peer in range(16):
        sent_ref[peer, :, D : D + 128] = high
        sent_ref[peer, :, D + 128 :] = low


def pack_kernel(
    place_hbm, shift_hbm, mask_hbm, rows_hbm, pixel_hbm,
    packed_ref, shift_rows_ref, mask_ref, pixel_ref,
    place_ref, shift_ref, rows_ref, sems,
):
    copies = [
        pltpu.make_async_copy(source, target, sems.at[at])
        for at, (source, target) in enumerate(
            [
                (rows_hbm, rows_ref),
                (place_hbm, place_ref),
                (shift_hbm, shift_ref),
                (mask_hbm, mask_ref),
                (pixel_hbm, pixel_ref),
            ]
        )
    ]
    for copy in copies:
        copy.start()
    copies[1].wait()
    slot = lax.broadcasted_iota(jnp.int32, (8, 128), 0)
    peers = rows_ref.shape[0]
    for peer in range(peers):
        places = jnp.zeros((8, 128), jnp.int32)
        for at in range(8):
            source = peer if at < 4 else (peer + 1) % peers
            places = jnp.where(slot == at, place_ref[at % 4, source], places)
        packed_ref[peer, :, D:] = places.astype(F32).astype(BF)
    copies[2].wait()
    shifts = jnp.zeros((8, 128), jnp.int32)
    for group in range(2):
        shifts = jnp.where(slot == group, shift_ref[0, group], shifts)
        shifts = jnp.where(slot == 2 + group, -((4 - shift_ref[1, group]) & 3), shifts)
    shift_rows_ref[...] = shifts
    copies[0].wait()
    rows = rows_ref[...].astype(F32)
    after = jnp.concatenate([rows[1:], rows[:1]], axis=0)
    packed_ref[:, :, :D] = jnp.concatenate([rows, after], axis=1).astype(BF)
    copies[3].wait()
    copies[4].wait()


def sinusoid(coordinate, channel_count):
    half_count = channel_count // 2
    lane = lax.broadcasted_iota(jnp.int32, (coordinate.shape[0], channel_count), 1)
    channel = jnp.where(lane < half_count, lane, lane - half_count).astype(F32)
    angles = coordinate.astype(F32) * jnp.exp(-math.log(10000.0) * channel / half_count)
    return jnp.where(lane < half_count, jnp.sin(angles), jnp.cos(angles))


def grid_coordinates(start, offsets_ref, first, total, channel_count):
    row = lax.broadcasted_iota(jnp.int32, (8, 128), 0)
    offset = jnp.where(row < 4, offsets_ref[first : first + 1], offsets_ref[first + 1 : first + 2])
    coordinate = start + (row & 3) - offset
    coordinate = jnp.where(coordinate < 0, coordinate + total, coordinate)
    coordinate = jnp.where(coordinate >= total, coordinate - total, coordinate)
    return jnp.concatenate([coordinate] * (channel_count // 128), axis=1)


def target_kernel(
    totals, shift_rows_ref, pixel_ref, own_ref, row_ref, last_row_ref, time_ref, frames_ref, rows_ref, columns_ref
):
    frames = grid_coordinates(lax.axis_index(TM) * 4, shift_rows_ref, 0, totals[0], 256)
    rows = grid_coordinates(lax.axis_index(ROW) * 4, shift_rows_ref, 2, totals[1], 384)
    frames_ref[...] = sinusoid(frames, 256)
    rows_ref[...] = sinusoid(rows, 384)
    columns_ref[...] = sinusoid(lax.broadcasted_iota(jnp.int32, (16, 384), 0), 384)
    second = jnp.concatenate([shift_rows_ref[2:3]] * (GROUP // 128), axis=1) == -1
    for frame in range(4):
        halo_ref, at_frame = (last_row_ref, 0) if frame == 3 else (row_ref, frame)
        for part in range(3):
            cols = slice(part * GROUP, part * GROUP + GROUP)
            picked = []
            for row in range(4):
                raw = pixel_ref[frame, row, :, cols].astype(F32)
                center = raw - lane_mean(raw)
                spread = jnp.sqrt(jnp.sum(center * center, axis=-1, keepdims=True) * (1.0 / (GROUP - 1)))
                target = center * (1.0 / (spread + 1e-06))
                own_ref[frame, row, :, cols] = target.astype(BF)
                if frame == 3:
                    time_ref[0, row, :, cols] = target.astype(BF)
                if row == 0:
                    halo_ref[at_frame, 0, :, cols] = target.astype(BF)
                if row in (1, 2):
                    picked.append(jnp.where(second, target[8:], target[:8]))
            halo_ref[at_frame, 1, :, cols] = jnp.concatenate(picked, axis=0).astype(BF)


def unpack_kernel(scale, back_ref, rows_ref, total_ref):
    rows = back_ref[:, :4, :D].astype(F32)
    before = back_ref[:, 4:, :D].astype(F32)
    before = jnp.concatenate([before[-1:], before[:-1]], axis=0)
    rows_ref[...] = (rows + before).astype(BF)
    sums = jnp.sum(back_ref[:, :, D:].astype(F32), axis=0)
    total_ref[...] = (sums[:, :128] + sums[:, 128:]) * scale


def shapes(*items):
    return [jax.ShapeDtypeStruct(dims, kind) for dims, kind in items]


def call(kernel, outputs, scratch, in_specs, limit):
    return pl.pallas_call(
        kernel,
        in_specs=in_specs,
        out_specs=[pl.BlockSpec(memory_space=VMEM)] * len(outputs),
        out_shape=shapes(*outputs),
        scratch_shapes=scratch,
        compiler_params=pltpu.CompilerParams(vmem_limit_bytes=limit << 20),
    )


def in_space(space, count):
    return [pl.BlockSpec(memory_space=space)] * count


def half_outputs(slots):
    return [
        ((HALF, D), BF),
        ((HALF, 3 * D), BF),
        ((HALF // WIN, PAIRS, WIN, 128), BF),
        ((HALF, 128), F32),
        ((slots, HALF), BF),
    ]


def pack_part(*operands):
    outputs = [((16, 8, D + 128), BF), ((8, 128), jnp.int32), ((8, 128), BF), ((4, 4, 16, PIX), BF)]
    scratch = [
        pltpu.SMEM((4, 16), jnp.int32),
        pltpu.SMEM((2, 2), jnp.int32),
        pltpu.VMEM((16, 4, D), BF),
        pltpu.SemaphoreType.DMA((5,)),
    ]
    return call(pack_kernel, outputs, scratch, in_space(HBM, 5), 8)(*operands)


def target_part(totals, *operands):
    outputs = [((frames, rows, 16, PIX), BF) for frames, rows in ((4, 4), (3, 2), (1, 2), (1, 4))]
    outputs += [((8, 256), F32), ((8, 384), F32), ((16, 384), F32)]
    kernel = functools.partial(target_kernel, totals)
    return call(kernel, outputs, [], in_space(VMEM, 2), 8)(*operands)


def early_part(*operands):
    outputs = half_outputs(SLOTS) + [((HALF, D), BF), ((D, 3 * D), BF), ((D, D), BF), ((D, PIX), BF)]
    scratch = [pltpu.VMEM((HALF, D), F32), pltpu.VMEM((HALF, D), BF), pltpu.SemaphoreType.DMA((5,))]
    return call(early_kernel, outputs, scratch, in_space(VMEM, 6) + in_space(HBM, 3), 20)(*operands)


def late_part(*operands):
    outputs = half_outputs(2 * SLOTS) + [((TOK, D), F32), ((TOK, 128), F32), ((TOK, PIX), F32)]
    scratch = [
        pltpu.VMEM((HALF, D), F32),
        pltpu.VMEM((HALF, D), BF),
        pltpu.VMEM((TOK, D), BF),
        pltpu.VMEM((TOK, D), F32),
        pltpu.VMEM((TOK, D), BF),
    ]
    return call(late_kernel, outputs, scratch, in_space(VMEM, 12), 26)(*operands)


def backward_part(*operands):
    outputs = [((SLOTS, D), BF), ((32, D), BF), ((8, 128), F32)]
    scratch = [
        pltpu.VMEM((5, 7, 16, PIX), BF),
        pltpu.VMEM((TOK, PIX), BF),
        pltpu.VMEM((TOK, D), BF),
        pltpu.VMEM((TOK, D), F32),
        pltpu.VMEM((TOK, D), F32),
        pltpu.VMEM((TOK, 3 * D), BF),
    ]
    return call(backward_kernel, outputs, scratch, in_space(SMEM, 1) + in_space(VMEM, 21), 34)(*operands)


def move(value, axis, steps):
    count = lax.axis_size(axis)
    return lax.ppermute(value, axis, [(at, (at + steps) % count) for at in range(count)])


def per_device(visible, slot_pos, window_shift, mask_token, w_qkv, w_out, w_head, pixels):
    frame_count, row_count = pixels.shape[:2]
    peers, slots = slot_pos.shape[2:]
    hold = functools.partial(pltpu.with_memory_space_constraint, memory_space=HBM)
    packed, shift_rows, mask_rows, near_pixels = pack_part(
        hold(slot_pos.reshape(peers, slots).T),
        hold(window_shift),
        hold(mask_token.reshape(8, 128)),
        hold(visible.reshape(peers, slots, D)),
        hold(pixels),
    )
    own = lax.all_to_all(packed, ROW, split_axis=0, concat_axis=0, tiled=True).reshape(SLOTS, D + 128)
    behind = move(own, TM, 1)
    frame_total = frame_count * lax.axis_size(TM)
    row_total = row_count * lax.axis_size(ROW)
    own_target, row_target, last_row_target, time_target, *positions = target_part(
        (frame_total, row_total), shift_rows, near_pixels
    )
    last_row_target = move(last_row_target, ROW, -1)
    row_target = move(row_target, ROW, -1)
    time_target = move(time_target, TM, 1)
    corner_target = move(last_row_target, TM, 1)

    tables = (mask_rows, *positions)
    *half_1, heads_1, w_qkv, w_out, w_head = early_part(
        shift_rows, own, *tables, hold(w_qkv), hold(w_out), hold(w_head)
    )
    *half_0, head_normed, head_scale, predicted = late_part(
        shift_rows, own, behind, *tables, half_1[0], heads_1, w_qkv, w_out, w_head
    )
    own_picked, behind_rows, local_total = backward_part(
        window_shift, *half_0, *half_1, head_normed, head_scale, predicted, w_qkv, w_out, w_head,
        own_target, row_target, last_row_target, time_target, corner_target,
    )
    other = move(local_total, "tm_1", 1)
    from_next = move(behind_rows, TM, -1)
    local_total = local_total + other
    turned = []
    for step in (1, 2, 3):
        turned.append(move(local_total, "tm_0", step))
    give = call(give_kernel, [((peers, 8, D + 256), BF)], [], in_space(VMEM, 8), 8)
    (sent,) = give(shift_rows, own, own_picked, from_next, local_total, *turned)
    back = lax.all_to_all(sent, ROW, split_axis=0, concat_axis=0, tiled=True)
    grad_scale = (frame_total * row_total * pixels.shape[2]) ** (-0.5)
    outputs = [((peers, slots, D), BF), ((8, 128), F32)]
    unpack = call(functools.partial(unpack_kernel, grad_scale), outputs, [], in_space(VMEM, 1), 8)
    d_visible, d_mask = unpack(back)
    return (d_visible.reshape(visible.shape), d_mask.reshape(D))


def solution(mesh):
    torus = Mesh(mesh.devices.reshape(4, 2, 4, 4), ALL)
    return jax.shard_map(
        per_device,
        mesh=torus,
        in_specs=(
            P(TM, ROW, None, None, None),
            P(TM, ROW, None, None),
            P(),
            P(),
            P(),
            P(),
            P(),
            P(TM, ROW, None, None),
        ),
        out_specs=(P(TM, ROW, None, None, None), P()),
        check_vma=False,
    )
```

profile of v0, /device:TPU:0, one launch (start us, length us, event | category | flops | bytes accessed | tf_op | source)
XLA Modules:
  0.0 72.6 jit_solution(1061658629392843241)
XLA Ops:
  0.6 1.3 %shard_map.95 = (bf16[16,8,1152]{2,1,0:T(8,128)(2,1)S(1)}, s32[8,128]{1,0:T(8,128)S(1)}, bf16[8,128]{1,0:T(8,128)(2,1)S(1)}, bf16[4,4,16,1536]{3,2,1,0:T(8,128)(2,1)S(1)}) custom-call(s32[4,16]{1,0:T(4,128)} %bitcast.13, s32[2,2]{1,0:T(2,128)} %shift_ref.1, bf16[8,128]{1,0:T(8,128)(2,1)} %bitcast.14, bf16[16,4,1024]{2,1,0:T(4,128)(2,1)} %bitcast.12, ...), custom_call_target="tpu_custom_call" | custom-call | tf_op jit(solution)/shard_map/pallas_call | solution.py:457
  1.9 16.0 %all_to_all.10 = bf16[16,8,1152]{2,1,0:T(8,128)(2,1)S(1)} all-to-all(bf16[16,8,1152]{2,1,0:T(8,128)(2,1)S(1)} %get-tuple-element.36), channel_id=1, replica_groups=mesh['tm_0'=4,'tm_1'=2,'row_0'=4,'row_1'=4] {'row_0','row_1'}, dimensions={0} | all-to-all | bytes 589824 | tf_op jit(solution)/shard_map/all_to_all | solution.py:514
  17.9 0.0 collective-permute-start
  17.9 0.9 %shard_map.96 = (bf16[4,4,16,1536]{3,2,1,0:T(8,128)(2,1)S(1)}, bf16[3,2,16,1536]{3,2,1,0:T(8,128)(2,1)S(1)}, bf16[1,2,16,1536]{3,2,1,0:T(8,128)(2,1)S(1)}, bf16[...) custom-call(s32[8,128]{1,0:T(8,128)S(1)} %get-tuple-element.35.shift_rows_, ...), custom_call_target="tpu_custom_call" | custom-call | tf_op jit(solution)/shard_map/pallas_call | solution.py:464
  18.8 1.3 %collective-permute-start.1 = (bf16[3,2,16,1536]{3,2,1,0:T(8,128)(2,1)S(1)}, bf16[3,2,16,1536]{3,2,1,0:T(8,128)(2,1)S(1)}, u32[]{:S(2)}, u32[]{:S(2)}) collective-permute-start(bf16[3,2,16,1536]{3,2,1,0:T(8,128)(2,1)S(1)} %get-tuple-element.60), channel_id=1, source_target_pairs={{0,15},{1,0},{2,1},{3,2},{4,3},{5,4},{6,5},{7,6},{8,7},{9,8},{10,9... | collective-permute-start | bytes 884744 | tf_op jit(solution)/shard_map/ppermute | solution.py:500
  20.2 0.8 %collective-permute-start.2 = (bf16[1,2,16,1536]{3,2,1,0:T(8,128)(2,1)S(1)}, bf16[1,2,16,1536]{3,2,1,0:T(8,128)(2,1)S(1)}, u32[]{:S(2)}, u32[]{:S(2)}) collective-permute-start(bf16[1,2,16,1536]{3,2,1,0:T(8,128)(2,1)S(1)} %get-tuple-element.61), channel_id=1, source_target_pairs={{0,15},{1,0},{2,1},{3,2},{4,3},{5,4},{6,5},{7,6},{8,7},{9,8},{10,9... | collective-permute-start | bytes 294920 | tf_op jit(solution)/shard_map/ppermute | solution.py:500
  20.9 1.5 %collective-permute-start.3 = (bf16[1,4,16,1536]{3,2,1,0:T(8,128)(2,1)S(1)}, bf16[1,4,16,1536]{3,2,1,0:T(8,128)(2,1)S(1)}, u32[]{:S(2)}, u32[]{:S(2)}) collective-permute-start(bf16[1,4,16,1536]{3,2,1,0:T(8,128)(2,1)S(1)} %get-tuple-element.62), channel_id=1, source_target_pairs={{0,16},{16,32},{32,48},{48,64},{64,80},{80,96},{96,112},{112,0},{1... | collective-permute-start | bytes 589832 | tf_op jit(solution)/shard_map/ppermute | solution.py:500
  22.4 7.4 %collective-permute-done.2.last_row_target = bf16[1,2,16,1536]{3,2,1,0:T(8,128)(2,1)S(1)} collective-permute-done((bf16[1,2,16,1536]{3,2,1,0:T(8,128)(2,1)S(1)}, bf16[1,2,16,1536]{3,2,1,0:T(8,128)(2,1)S(1)}, u32[]{:S(2)}, u32[]{:S(2)}) %collective-permute-start.2) | collective-permute-done | bytes 98336 | tf_op jit(solution)/shard_map/ppermute | solution.py:500
  29.8 0.9 %collective-permute-start.4 = (bf16[1,2,16,1536]{3,2,1,0:T(8,128)(2,1)S(1)}, bf16[1,2,16,1536]{3,2,1,0:T(8,128)(2,1)S(1)}, u32[]{:S(2)}, u32[]{:S(2)}) collective-permute-start(bf16[1,2,16,1536]{3,2,1,0:T(8,128)(2,1)S(1)} %collective-permute-done.2.last_row_target), channel_id=1, source_target_pairs={{0,16},{16,32},{32,48},{48,64},{64,80},{80,96},{96,112},{112,0},{1... | collective-permute-start | bytes 294920 | tf_op jit(solution)/shard_map/ppermute | solution.py:500
  30.7 4.5 %shard_map.97 = (bf16[128,1024]{1,0:T(8,128)(2,1)S(1)}, bf16[128,3072]{1,0:T(8,128)(2,1)S(1)}, bf16[2,8,64,128]{3,2,1,0:T(8,128)(2,1)S(1)}, f32[128,128]{1,0:T(8...) custom-call(s32[8,128]{1,0:T(8,128)S(1)} %get-tuple-element.35.shift, ...), custom_call_target="tpu_custom_call" | custom-call | tf_op jit(solution)/shard_map/pallas_call | solution.py:470
  35.3 0.0 collective-permute-done.behind_ref
  35.3 0.0 copy-start
  35.3 4.2 %shard_map.98 = (bf16[128,1024]{1,0:T(8,128)(2,1)S(1)}, bf16[128,3072]{1,0:T(8,128)(2,1)S(1)}, bf16[2,8,64,128]{3,2,1,0:T(8,128)(2,1)S(1)}, f32[128,128]{1,0:T(8...) custom-call(s32[8,128]{1,0:T(8,128)S(1)} %get-tuple-element.35.shift, ...), custom_call_target="tpu_custom_call" | custom-call | tf_op jit(solution)/shard_map/pallas_call | solution.py:482
  39.5 0.0 collective-permute-done.4.corner_target
  39.5 0.0 collective-permute-done.3.time_target
  39.5 0.0 collective-permute-done.1.row_target
  39.5 0.0 copy-done
  39.5 6.7 %shard_map.99 = (bf16[128,1024]{1,0:T(8,128)(2,1)S(1)}, bf16[32,1024]{1,0:T(8,128)(2,1)S(1)}, f32[8,128]{1,0:T(8,128)S(1)}) custom-call(s32[2,2]{1,0:T(2,128)S(1)} %copy-done, bf16[128,1024]{1,0:T(8,128)(2,1)S(1)} %get-tuple-element.47.embedded_0_ref, bf16[128,3072]{1,0:T(8,128)(2,1)S(1)} %get-tuple-element.48.qkv_0_ref, ...), custom_call_target="tpu_custom_call" | custom-call | tf_op jit(solution)/shard_map/pallas_call | solution.py:495
  46.2 2.1 %collective-permute-start.5 = (bf16[32,1024]{1,0:T(8,128)(2,1)S(1)}, bf16[32,1024]{1,0:T(8,128)(2,1)S(1)}, u32[]{:S(2)}, u32[]{:S(2)}) collective-permute-start(bf16[32,1024]{1,0:T(8,128)(2,1)S(1)} %get-tuple-element.64), channel_id=1, source_target_pairs={{0,112},{16,0},{32,16},{48,32},{64,48},{80,64},{96,80},{112,96},{1... | collective-permute-start | bytes 196616 | tf_op jit(solution)/shard_map/ppermute | solution.py:500
  48.3 0.0 collective-permute-start.6
  48.3 1.2 %collective-permute-done.6 = f32[8,128]{1,0:T(8,128)S(1)} collective-permute-done((f32[8,128]{1,0:T(8,128)S(1)}, f32[8,128]{1,0:T(8,128)S(1)}, u32[]{:S(2)}, u32[]{:S(2)}) %collective-permute-start.6) | collective-permute-done | bytes 4128 | tf_op jit(solution)/shard_map/ppermute | solution.py:500
  49.5 1.0 %collective-permute-start.7 = (f32[8,128]{1,0:T(8,128)S(1)}, f32[8,128]{1,0:T(8,128)S(1)}, u32[]{:S(2)}, u32[]{:S(2)}) collective-permute-start(f32[8,128]{1,0:T(8,128)S(1)} %add.3.total_ref), channel_id=1, source_target_pairs={{0,32},{32,64},{64,96},{96,0},{1,33},{33,65},{65,97},{97,1},{2,34}... | collective-permute-start | bytes 12296 | tf_op jit(solution)/shard_map/ppermute | solution.py:500
  50.5 2.6 %collective-permute-start.8 = (f32[8,128]{1,0:T(8,128)S(1)}, f32[8,128]{1,0:T(8,128)S(1)}, u32[]{:S(2)}, u32[]{:S(2)}) collective-permute-start(f32[8,128]{1,0:T(8,128)S(1)} %add.3.total_ref), channel_id=1, source_target_pairs={{0,64},{32,96},{64,0},{96,32},{1,65},{33,97},{65,1},{97,33},{2,66}... | collective-permute-start | bytes 12296 | tf_op jit(solution)/shard_map/ppermute | solution.py:500
  53.1 1.9 %collective-permute-start.9 = (f32[8,128]{1,0:T(8,128)S(1)}, f32[8,128]{1,0:T(8,128)S(1)}, u32[]{:S(2)}, u32[]{:S(2)}) collective-permute-start(f32[8,128]{1,0:T(8,128)S(1)} %add.3.total_ref), channel_id=1, source_target_pairs={{0,96},{32,0},{64,32},{96,64},{1,97},{33,1},{65,33},{97,65},{2,98}... | collective-permute-start | bytes 12296 | tf_op jit(solution)/shard_map/ppermute | solution.py:500
  55.1 0.0 collective-permute-done.7.turned_1_ref
  55.1 0.6 collective-permute-done.8.turned_2_ref
  55.6 1.1 %collective-permute-done.9.turned_3_ref = f32[8,128]{1,0:T(8,128)S(1)} collective-permute-done((f32[8,128]{1,0:T(8,128)S(1)}, f32[8,128]{1,0:T(8,128)S(1)}, u32[]{:S(2)}, u32[]{:S(2)}) %collective-permute-start.9) | collective-permute-done | bytes 4128 | tf_op jit(solution)/shard_map/ppermute | solution.py:500
  56.8 0.0 collective-permute-done.5.next_ref
  56.8 0.2 shard_map.100
  57.0 14.8 %all_to_all.11.back_ref = bf16[16,8,1280]{2,1,0:T(8,128)(2,1)S(1)} all-to-all(bf16[16,8,1280]{2,1,0:T(8,128)(2,1)S(1)} %shard_map.100), channel_id=1, replica_groups=mesh['tm_0'=4,'tm_1'=2,'row_0'=4,'row_1'=4] {'row_0','row_1'}, dimensions={0} | all-to-all | bytes 655360 | tf_op jit(solution)/shard_map/all_to_all | solution.py:545
  71.8 0.8 %shard_map.101 = (bf16[16,4,1024]{2,1,0:T(4,128)(2,1)}, f32[8,128]{1,0:T(8,128)}) custom-call(bf16[16,8,1280]{2,1,0:T(8,128)(2,1)S(1)} %all_to_all.11.back_ref), custom_call_target="tpu_custom_call" | custom-call | tf_op jit(solution)/shard_map/pallas_call | solution.py:549
  (1 shorter events, 0.0 us)
Async XLA Ops:
  17.9 17.4 %collective-permute-start = (bf16[128,1152]{1,0:T(8,128)(2,1)S(1)}, bf16[128,1152]{1,0:T(8,128)(2,1)S(1)}, u32[]{:S(2)}, u32[]{:S(2)}) collective-permute-start(bf16[128,1152]{1,0:T(8,128)(2,1)S(1)} %bitcast.8), channel_id=1, source_target_pairs={{0,16},{16,32},{32,48},{48,64},{64,80},{80,96},{96,112},{112,0},{1... | collective-permute-start | bytes 884744 | tf_op jit(solution)/shard_map/ppermute | solution.py:500
  18.8 20.7 %collective-permute-start.1 = (bf16[3,2,16,1536]{3,2,1,0:T(8,128)(2,1)S(1)}, bf16[3,2,16,1536]{3,2,1,0:T(8,128)(2,1)S(1)}, u32[]{:S(2)}, u32[]{:S(2)}) collective-permute-start(bf16[3,2,16,1536]{3,2,1,0:T(8,128)(2,1)S(1)} %get-tuple-element.60), channel_id=1, source_target_pairs={{0,15},{1,0},{2,1},{3,2},{4,3},{5,4},{6,5},{7,6},{8,7},{9,8},{10,9... | collective-permute-start | bytes 884744 | tf_op jit(solution)/shard_map/ppermute | solution.py:500
  20.2 9.7 %collective-permute-start.2 = (bf16[1,2,16,1536]{3,2,1,0:T(8,128)(2,1)S(1)}, bf16[1,2,16,1536]{3,2,1,0:T(8,128)(2,1)S(1)}, u32[]{:S(2)}, u32[]{:S(2)}) collective-permute-start(bf16[1,2,16,1536]{3,2,1,0:T(8,128)(2,1)S(1)} %get-tuple-element.61), channel_id=1, source_target_pairs={{0,15},{1,0},{2,1},{3,2},{4,3},{5,4},{6,5},{7,6},{8,7},{9,8},{10,9... | collective-permute-start | bytes 294920 | tf_op jit(solution)/shard_map/ppermute | solution.py:500
  20.9 18.5 %collective-permute-start.3 = (bf16[1,4,16,1536]{3,2,1,0:T(8,128)(2,1)S(1)}, bf16[1,4,16,1536]{3,2,1,0:T(8,128)(2,1)S(1)}, u32[]{:S(2)}, u32[]{:S(2)}) collective-permute-start(bf16[1,4,16,1536]{3,2,1,0:T(8,128)(2,1)S(1)} %get-tuple-element.62), channel_id=1, source_target_pairs={{0,16},{16,32},{32,48},{48,64},{64,80},{80,96},{96,112},{112,0},{1... | collective-permute-start | bytes 589832 | tf_op jit(solution)/shard_map/ppermute | solution.py:500
  29.8 9.6 %collective-permute-start.4 = (bf16[1,2,16,1536]{3,2,1,0:T(8,128)(2,1)S(1)}, bf16[1,2,16,1536]{3,2,1,0:T(8,128)(2,1)S(1)}, u32[]{:S(2)}, u32[]{:S(2)}) collective-permute-start(bf16[1,2,16,1536]{3,2,1,0:T(8,128)(2,1)S(1)} %collective-permute-done.2.last_row_target), channel_id=1, source_target_pairs={{0,16},{16,32},{32,48},{48,64},{64,80},{80,96},{96,112},{112,0},{1... | collective-permute-start | bytes 294920 | tf_op jit(solution)/shard_map/ppermute | solution.py:500
  35.3 4.2 %copy-start = (s32[2,2]{1,0:T(2,128)S(1)}, s32[2,2]{1,0:T(2,128)}, u32[]{:S(2)}) copy-start(s32[2,2]{1,0:T(2,128)} %shift_ref.1) | copy-start | bytes 52
  46.2 10.6 %collective-permute-start.5 = (bf16[32,1024]{1,0:T(8,128)(2,1)S(1)}, bf16[32,1024]{1,0:T(8,128)(2,1)S(1)}, u32[]{:S(2)}, u32[]{:S(2)}) collective-permute-start(bf16[32,1024]{1,0:T(8,128)(2,1)S(1)} %get-tuple-element.64), channel_id=1, source_target_pairs={{0,112},{16,0},{32,16},{48,32},{64,48},{80,64},{96,80},{112,96},{1... | collective-permute-start | bytes 196616 | tf_op jit(solution)/shard_map/ppermute | solution.py:500
  48.3 1.2 %collective-permute-start.6 = (f32[8,128]{1,0:T(8,128)S(1)}, f32[8,128]{1,0:T(8,128)S(1)}, u32[]{:S(2)}, u32[]{:S(2)}) collective-permute-start(f32[8,128]{1,0:T(8,128)S(1)} %get-tuple-element.65), channel_id=1, source_target_pairs={{0,16},{16,0},{1,17},{17,1},{2,18},{18,2},{3,19},{19,3},{4,20},{20... | collective-permute-start | bytes 12296 | tf_op jit(solution)/shard_map/ppermute | solution.py:500
  49.5 5.6 %collective-permute-start.7 = (f32[8,128]{1,0:T(8,128)S(1)}, f32[8,128]{1,0:T(8,128)S(1)}, u32[]{:S(2)}, u32[]{:S(2)}) collective-permute-start(f32[8,128]{1,0:T(8,128)S(1)} %add.3.total_ref), channel_id=1, source_target_pairs={{0,32},{32,64},{64,96},{96,0},{1,33},{33,65},{65,97},{97,1},{2,34}... | collective-permute-start | bytes 12296 | tf_op jit(solution)/shard_map/ppermute | solution.py:500
  50.5 5.1 %collective-permute-start.8 = (f32[8,128]{1,0:T(8,128)S(1)}, f32[8,128]{1,0:T(8,128)S(1)}, u32[]{:S(2)}, u32[]{:S(2)}) collective-permute-start(f32[8,128]{1,0:T(8,128)S(1)} %add.3.total_ref), channel_id=1, source_target_pairs={{0,64},{32,96},{64,0},{96,32},{1,65},{33,97},{65,1},{97,33},{2,66}... | collective-permute-start | bytes 12296 | tf_op jit(solution)/shard_map/ppermute | solution.py:500
  53.1 3.6 %collective-permute-start.9 = (f32[8,128]{1,0:T(8,128)S(1)}, f32[8,128]{1,0:T(8,128)S(1)}, u32[]{:S(2)}, u32[]{:S(2)}) collective-permute-start(f32[8,128]{1,0:T(8,128)S(1)} %add.3.total_ref), channel_id=1, source_target_pairs={{0,96},{32,0},{64,32},{96,64},{1,97},{33,1},{65,33},{97,65},{2,98}... | collective-permute-start | bytes 12296 | tf_op jit(solution)/shard_map/ppermute | solution.py:500
where the time goes:
time: 72.8 us; the launch traced here: 72.6 us
  blocking collectives  30.8 us (42%)
  Pallas kernels  18.6 us (26%)
  starting transfers between devices  12.1 us (17%)
  waiting for transfers between devices  10.3 us (14%)
  between operations  0.73 us (1%)
    all_to_all x1, blocking collectives, per_device(): lax.all_to_all(packed, ROW, split_axis=0, concat_axis=0, tiled=True)  16 us
    all_to_all x1, blocking collectives, per_device(): back = lax.all_to_all(sent, ROW, split_axis=0, concat_axis=0, tiled=True)  14.8 us
    ppermute x10, starting transfers between devices, move(): lax.ppermute(value, axis, [(at, (at + steps) % count) for at in range(cou...  12.1 us
    ppermute x10, waiting for transfers between devices, move(): lax.ppermute(value, axis, [(at, (at + steps) % count) for at in range(cou...  10.3 us
    pallas_call x1, Pallas kernels, backward_part(): call(backward_kernel, outputs, scratch, in_space(SMEM, 1) + in_space(VMEM...  6.7 us
    pallas_call x1, Pallas kernels, early_part(): call(early_kernel, outputs, scratch, in_space(VMEM, 6) + in_space(HBM, 3)...  4.54 us
    pallas_call x1, Pallas kernels, late_part(): call(late_kernel, outputs, scratch, in_space(VMEM, 12), 26)(*operands)  4.17 us
  transfers between devices with their start and end apart: 10, of which 4 were waited for; matrix products, arithmetic and copies ran while one was open for 0% of the time, Pallas kernels for 13%

commit v1 on v0

--- a/solution.py
+++ b/solution.py
@@ -111,21 +111,21 @@
 
 
 def attend(qkv_ref, probs_ref, heads_ref):
-    for window in range(HALF // WIN):
-        rows = slice(window * WIN, window * WIN + WIN)
-        scores = []
-        for pair in range(PAIRS):
-            q = qkv_ref[rows, pair * 128 : pair * 128 + 128]
-            k = qkv_ref[rows, D + pair * 128 : D + pair * 128 + 128]
-            scores.append(dot(k, two_heads(q), NT_DIMS) * 0.125)
-        probs = []
-        for pair in range(PAIRS):
-            weights = jnp.exp(scores[pair] - jnp.max(scores[pair], axis=0, keepdims=True))
-            probs.append((weights * (1.0 / jnp.sum(weights, axis=0, keepdims=True))).astype(BF))
-            probs_ref[window, pair] = probs[pair]
-        for pair in range(PAIRS):
-            v = qkv_ref[rows, 2 * D + pair * 128 : 2 * D + pair * 128 + 128]
-            heads_ref[rows, pair * 128 : pair * 128 + 128] = own_head(dot(probs[pair], v, TN_DIMS)).astype(BF)
+    units = [(window, pair) for window in range(HALF // WIN) for pair in range(PAIRS)]
+    rows = [slice(window * WIN, window * WIN + WIN) for window, pair in units]
+    scores = []
+    for at, (window, pair) in enumerate(units):
+        q = qkv_ref[rows[at], pair * 128 : pair * 128 + 128]
+        k = qkv_ref[rows[at], D + pair * 128 : D + pair * 128 + 128]
+        scores.append(dot(k, two_heads(q), NT_DIMS) * 0.125)
+    probs = []
+    for at, unit in enumerate(units):
+        weights = jnp.exp(scores[at] - jnp.max(scores[at], axis=0, keepdims=True))
+        probs.append((weights * (1.0 / jnp.sum(weights, axis=0, keepdims=True))).astype(BF))
+        probs_ref[unit] = probs[at]
+    for at, (window, pair) in enumerate(units):
+        v = qkv_ref[rows[at], 2 * D + pair * 128 : 2 * D + pair * 128 + 128]
+        heads_ref[rows[at], pair * 128 : pair * 128 + 128] = own_head(dot(probs[at], v, TN_DIMS)).astype(BF)
 
 
 def early_kernel(
@@ -245,32 +245,32 @@
 
     narrow_ref[...] = dot(narrow_ref[...], w_out_ref[...], NT_DIMS).astype(BF)
 
-    for window in range(TOK // WIN):
-        rows = slice(window * WIN, window * WIN + WIN)
-        frame_pair, group = divmod(window, 2)
-        local = slice(group * WIN, group * WIN + WIN)
+    for frame_pair in range(2):
         qkv_ref = qkv_refs[frame_pair]
         probs_ref = probs_refs[frame_pair]
-        cols = [[slice(at * D + pair * 128, at * D + pair * 128 + 128) for at in range(3)] for pair in range(PAIRS)]
+        units = [(group, pair) for group in range(2) for pair in range(PAIRS)]
+        local = [slice(group * WIN, group * WIN + WIN) for group, pair in units]
+        rows = [slice((frame_pair * 2 + group) * WIN, (frame_pair * 2 + group + 1) * WIN) for group, pair in units]
+        cols = [[slice(at * D + pair * 128, at * D + pair * 128 + 128) for at in range(3)] for group, pair in units]
         d_probs = []
         out_heads = []
-        for pair in range(PAIRS):
-            out_heads.append(two_heads(narrow_ref[rows, cols[pair][0]]))
-            d_probs.append(dot(qkv_ref[local, cols[pair][2]], out_heads[pair], NT_DIMS))
-        for pair in range(PAIRS):
-            dqkv_ref[rows, cols[pair][2]] = dot(probs_ref[group, pair], out_heads[pair], NN_DIMS).astype(BF)
+        for at, unit in enumerate(units):
+            out_heads.append(two_heads(narrow_ref[rows[at], cols[at][0]]))
+            d_probs.append(dot(qkv_ref[local[at], cols[at][2]], out_heads[at], NT_DIMS))
+        for at, unit in enumerate(units):
+            dqkv_ref[rows[at], cols[at][2]] = dot(probs_ref[unit], out_heads[at], NN_DIMS).astype(BF)
         d_scores = []
-        for pair in range(PAIRS):
-            probs = probs_ref[group, pair].astype(F32)
-            cotangent = d_probs[pair].astype(BF).astype(F32)
+        for at, unit in enumerate(units):
+            probs = probs_ref[unit].astype(F32)
+            cotangent = d_probs[at].astype(BF).astype(F32)
             mean = jnp.sum(cotangent * probs, axis=0, keepdims=True)
             d_scores.append((probs * (cotangent - mean) * 0.125).astype(BF))
-        for pair in range(PAIRS):
-            q_heads = two_heads(qkv_ref[local, cols[pair][0]])
-            dqkv_ref[rows, cols[pair][1]] = dot(d_scores[pair], q_heads, NN_DIMS).astype(BF)
-        for pair in range(PAIRS):
-            d_q = own_head(dot(d_scores[pair], qkv_ref[local, cols[pair][1]], TN_DIMS))
-            dqkv_ref[rows, cols[pair][0]] = d_q.astype(BF)
+        for at, unit in enumerate(units):
+            q_heads = two_heads(qkv_ref[local[at], cols[at][0]])
+            dqkv_ref[rows[at], cols[at][1]] = dot(d_scores[at], q_heads, NN_DIMS).astype(BF)
+        for at, unit in enumerate(units):
+            d_q = own_head(dot(d_scores[at], qkv_ref[local[at], cols[at][1]], TN_DIMS))
+            dqkv_ref[rows[at], cols[at][0]] = d_q.astype(BF)
 
     for part in range(2):
         cols = slice(part * 512, part * 512 + 512)
@@ -321,8 +321,8 @@
 
 
 def pack_kernel(
-    place_hbm, shift_hbm, mask_hbm, rows_hbm, pixel_hbm,
-    packed_ref, shift_rows_ref, mask_ref, pixel_ref,
+    place_hbm, shift_hbm, mask_hbm, rows_hbm,
+    packed_ref, shift_rows_ref, mask_ref,
     place_ref, shift_ref, rows_ref, sems,
 ):
     copies = [
@@ -333,7 +333,6 @@
                 (place_hbm, place_ref),
                 (shift_hbm, shift_ref),
                 (mask_hbm, mask_ref),
-                (pixel_hbm, pixel_ref),
             ]
         )
     ]
@@ -359,7 +358,6 @@
     after = jnp.concatenate([rows[1:], rows[:1]], axis=0)
     packed_ref[:, :, :D] = jnp.concatenate([rows, after], axis=1).astype(BF)
     copies[3].wait()
-    copies[4].wait()
 
 
 def sinusoid(coordinate, channel_count):
@@ -380,8 +378,12 @@
 
 
 def target_kernel(
-    totals, shift_rows_ref, pixel_ref, own_ref, row_ref, last_row_ref, time_ref, frames_ref, rows_ref, columns_ref
+    totals, shift_rows_ref, pixel_hbm, own_ref, row_ref, last_row_ref, time_ref, frames_ref, rows_ref, columns_ref,
+    pixel_ref, sems,
 ):
+    copies = [pltpu.make_async_copy(pixel_hbm.at[at], pixel_ref.at[at], sems.at[at]) for at in range(4)]
+    for copy in copies:
+        copy.start()
     frames = grid_coordinates(lax.axis_index(TM) * 4, shift_rows_ref, 0, totals[0], 256)
     rows = grid_coordinates(lax.axis_index(ROW) * 4, shift_rows_ref, 2, totals[1], 384)
     frames_ref[...] = sinusoid(frames, 256)
@@ -389,6 +391,7 @@
     columns_ref[...] = sinusoid(lax.broadcasted_iota(jnp.int32, (16, 384), 0), 384)
     second = jnp.concatenate([shift_rows_ref[2:3]] * (GROUP // 128), axis=1) == -1
     for frame in range(4):
+        copies[frame].wait()
         halo_ref, at_frame = (last_row_ref, 0) if frame == 3 else (row_ref, frame)
         for part in range(3):
             cols = slice(part * GROUP, part * GROUP + GROUP)
@@ -447,21 +450,22 @@
 
 
 def pack_part(*operands):
-    outputs = [((16, 8, D + 128), BF), ((8, 128), jnp.int32), ((8, 128), BF), ((4, 4, 16, PIX), BF)]
+    outputs = [((16, 8, D + 128), BF), ((8, 128), jnp.int32), ((8, 128), BF)]
     scratch = [
         pltpu.SMEM((4, 16), jnp.int32),
         pltpu.SMEM((2, 2), jnp.int32),
         pltpu.VMEM((16, 4, D), BF),
-        pltpu.SemaphoreType.DMA((5,)),
+        pltpu.SemaphoreType.DMA((4,)),
     ]
-    return call(pack_kernel, outputs, scratch, in_space(HBM, 5), 8)(*operands)
+    return call(pack_kernel, outputs, scratch, in_space(HBM, 4), 8)(*operands)
 
 
 def target_part(totals, *operands):
     outputs = [((frames, rows, 16, PIX), BF) for frames, rows in ((4, 4), (3, 2), (1, 2), (1, 4))]
     outputs += [((8, 256), F32), ((8, 384), F32), ((16, 384), F32)]
     kernel = functools.partial(target_kernel, totals)
-    return call(kernel, outputs, [], in_space(VMEM, 2), 8)(*operands)
+    scratch = [pltpu.VMEM((4, 4, 16, PIX), BF), pltpu.SemaphoreType.DMA((4,))]
+    return call(kernel, outputs, scratch, in_space(VMEM, 1) + in_space(HBM, 1), 8)(*operands)
 
 
 def early_part(*operands):
@@ -504,19 +508,18 @@
     frame_count, row_count = pixels.shape[:2]
     peers, slots = slot_pos.shape[2:]
     hold = functools.partial(pltpu.with_memory_space_constraint, memory_space=HBM)
-    packed, shift_rows, mask_rows, near_pixels = pack_part(
+    packed, shift_rows, mask_rows = pack_part(
         hold(slot_pos.reshape(peers, slots).T),
         hold(window_shift),
         hold(mask_token.reshape(8, 128)),
         hold(visible.reshape(peers, slots, D)),
-        hold(pixels),
     )
     own = lax.all_to_all(packed, ROW, split_axis=0, concat_axis=0, tiled=True).reshape(SLOTS, D + 128)
     behind = move(own, TM, 1)
     frame_total = frame_count * lax.axis_size(TM)
     row_total = row_count * lax.axis_size(ROW)
     own_target, row_target, last_row_target, time_target, *positions = target_part(
-        (frame_total, row_total), shift_rows, near_pixels
+        (frame_total, row_total), shift_rows, hold(pixels)
     )
     last_row_target = move(last_row_target, ROW, -1)
     row_target = move(row_target, ROW, -1)

time: 72.8 us -> 73.3 us (level)
  transfers between devices with their start and end apart: 10 -> 10, of which waited for: 4 -> 4; matrix products, arithmetic and copies ran while one was open for 0% -> 0% of each run, Pallas kernels for 13% -> 14%
where the time goes in v1:
time: 73.3 us; the launch traced here: 73 us
  blocking collectives  30.8 us (42%)
  Pallas kernels  19.1 us (26%)
  starting transfers between devices  12.1 us (17%)
  waiting for transfers between devices  10.3 us (14%)
    all_to_all x1, blocking collectives, per_device(): lax.all_to_all(packed, ROW, split_axis=0, concat_axis=0, tiled=True)  16 us
    all_to_all x1, blocking collectives, per_device(): back = lax.all_to_all(sent, ROW, split_axis=0, concat_axis=0, tiled=True)  14.8 us
    ppermute x10, starting transfers between devices, move(): lax.ppermute(value, axis, [(at, (at + steps) % count) for at in range(cou...  12.1 us
    ppermute x10, waiting for transfers between devices, move(): lax.ppermute(value, axis, [(at, (at + steps) % count) for at in range(cou...  10.3 us
    pallas_call x1, Pallas kernels, backward_part(): call(backward_kernel, outputs, scratch, in_space(SMEM, 1) + in_space(VMEM...  6.65 us
    pallas_call x1, Pallas kernels, early_part(): call(early_kernel, outputs, scratch, in_space(VMEM, 6) + in_space(HBM, 3)...  4.54 us
    pallas_call x1, Pallas kernels, late_part(): call(late_kernel, outputs, scratch, in_space(VMEM, 12), 26)(*operands)  3.97 us
    pallas_call x1, Pallas kernels, target_part(): call(kernel, outputs, scratch, in_space(VMEM, 1) + in_space(HBM, 1), 8)  1.93 us
  transfers between devices with their start and end apart: 10, of which 4 were waited for; matrix products, arithmetic and copies ran while one was open for 0% of the time, Pallas kernels for 14%

profile of v1, /device:TPU:0, one launch (start us, length us, event | category | flops | bytes accessed | tf_op | source)
XLA Modules:
  0.0 73.0 jit_solution(12616626723750692418)
XLA Ops:
  0.6 1.0 %shard_map.95 = (bf16[16,8,1152]{2,1,0:T(8,128)(2,1)S(1)}, s32[8,128]{1,0:T(8,128)S(1)}, bf16[8,128]{1,0:T(8,128)(2,1)S(1)}) custom-call(s32[4,16]{1,0:T(4,128)} %bitcast.13, s32[2,2]{1,0:T(2,128)} %shift_ref.1, bf16[8,128]{1,0:T(8,128)(2,1)} %bitcast.14, bf16[16,4,1024]{2,1,0:T(4,128)(2,1)} %bitcast.12), custom_call_target="tpu_custom_call" | custom-call | tf_op jit(solution)/shard_map/pallas_call | solution.py:460
  1.6 16.0 %all_to_all.10 = bf16[16,8,1152]{2,1,0:T(8,128)(2,1)S(1)} all-to-all(bf16[16,8,1152]{2,1,0:T(8,128)(2,1)S(1)} %get-tuple-element.35), channel_id=1, replica_groups=mesh['tm_0'=4,'tm_1'=2,'row_0'=4,'row_1'=4] {'row_0','row_1'}, dimensions={0} | all-to-all | bytes 589824 | tf_op jit(solution)/shard_map/all_to_all | solution.py:517
  17.6 0.0 collective-permute-start
  17.6 1.9 %shard_map.96 = (bf16[4,4,16,1536]{3,2,1,0:T(8,128)(2,1)S(1)}, bf16[3,2,16,1536]{3,2,1,0:T(8,128)(2,1)S(1)}, bf16[1,2,16,1536]{3,2,1,0:T(8,128)(2,1)S(1)}, bf16[...) custom-call(s32[8,128]{1,0:T(8,128)S(1)} %get-tuple-element.34.shift_rows_, ...), custom_call_target="tpu_custom_call" | custom-call | tf_op jit(solution)/shard_map/pallas_call | solution.py:468
  19.6 1.3 %collective-permute-start.1 = (bf16[3,2,16,1536]{3,2,1,0:T(8,128)(2,1)S(1)}, bf16[3,2,16,1536]{3,2,1,0:T(8,128)(2,1)S(1)}, u32[]{:S(2)}, u32[]{:S(2)}) collective-permute-start(bf16[3,2,16,1536]{3,2,1,0:T(8,128)(2,1)S(1)} %get-tuple-element.58), channel_id=1, source_target_pairs={{0,15},{1,0},{2,1},{3,2},{4,3},{5,4},{6,5},{7,6},{8,7},{9,8},{10,9... | collective-permute-start | bytes 884744 | tf_op jit(solution)/shard_map/ppermute | solution.py:504
  20.9 0.8 %collective-permute-start.2 = (bf16[1,2,16,1536]{3,2,1,0:T(8,128)(2,1)S(1)}, bf16[1,2,16,1536]{3,2,1,0:T(8,128)(2,1)S(1)}, u32[]{:S(2)}, u32[]{:S(2)}) collective-permute-start(bf16[1,2,16,1536]{3,2,1,0:T(8,128)(2,1)S(1)} %get-tuple-element.59), channel_id=1, source_target_pairs={{0,15},{1,0},{2,1},{3,2},{4,3},{5,4},{6,5},{7,6},{8,7},{9,8},{10,9... | collective-permute-start | bytes 294920 | tf_op jit(solution)/shard_map/ppermute | solution.py:504
  21.7 1.5 %collective-permute-start.3 = (bf16[1,4,16,1536]{3,2,1,0:T(8,128)(2,1)S(1)}, bf16[1,4,16,1536]{3,2,1,0:T(8,128)(2,1)S(1)}, u32[]{:S(2)}, u32[]{:S(2)}) collective-permute-start(bf16[1,4,16,1536]{3,2,1,0:T(8,128)(2,1)S(1)} %get-tuple-element.60), channel_id=1, source_target_pairs={{0,16},{16,32},{32,48},{48,64},{64,80},{80,96},{96,112},{112,0},{1... | collective-permute-start | bytes 589832 | tf_op jit(solution)/shard_map/ppermute | solution.py:504
  23.1 7.4 %collective-permute-done.2.last_row_target = bf16[1,2,16,1536]{3,2,1,0:T(8,128)(2,1)S(1)} collective-permute-done((bf16[1,2,16,1536]{3,2,1,0:T(8,128)(2,1)S(1)}, bf16[1,2,16,1536]{3,2,1,0:T(8,128)(2,1)S(1)}, u32[]{:S(2)}, u32[]{:S(2)}) %collective-permute-start.2) | collective-permute-done | bytes 98336 | tf_op jit(solution)/shard_map/ppermute | solution.py:504
  30.6 0.9 %collective-permute-start.4 = (bf16[1,2,16,1536]{3,2,1,0:T(8,128)(2,1)S(1)}, bf16[1,2,16,1536]{3,2,1,0:T(8,128)(2,1)S(1)}, u32[]{:S(2)}, u32[]{:S(2)}) collective-permute-start(bf16[1,2,16,1536]{3,2,1,0:T(8,128)(2,1)S(1)} %collective-permute-done.2.last_row_target), channel_id=1, source_target_pairs={{0,16},{16,32},{32,48},{48,64},{64,80},{80,96},{96,112},{112,0},{1... | collective-permute-start | bytes 294920 | tf_op jit(solution)/shard_map/ppermute | solution.py:504
  31.4 4.5 %shard_map.97 = (bf16[128,1024]{1,0:T(8,128)(2,1)S(1)}, bf16[128,3072]{1,0:T(8,128)(2,1)S(1)}, bf16[2,8,64,128]{3,2,1,0:T(8,128)(2,1)S(1)}, f32[128,128]{1,0:T(8...) custom-call(s32[8,128]{1,0:T(8,128)S(1)} %get-tuple-element.34.shift, ...), custom_call_target="tpu_custom_call" | custom-call | tf_op jit(solution)/shard_map/pallas_call | solution.py:474
  36.0 0.0 collective-permute-done.behind_ref
  36.0 0.0 copy-start
  36.0 4.0 %shard_map.98 = (bf16[128,1024]{1,0:T(8,128)(2,1)S(1)}, bf16[128,3072]{1,0:T(8,128)(2,1)S(1)}, bf16[2,8,64,128]{3,2,1,0:T(8,128)(2,1)S(1)}, f32[128,128]{1,0:T(8...) custom-call(s32[8,128]{1,0:T(8,128)S(1)} %get-tuple-element.34.shift, ...), custom_call_target="tpu_custom_call" | custom-call | tf_op jit(solution)/shard_map/pallas_call | solution.py:486
  40.0 0.0 collective-permute-done.4.corner_target
  40.0 0.0 collective-permute-done.3.time_target
  40.0 0.0 collective-permute-done.1.row_target
  40.0 0.0 copy-done
  40.0 6.7 %shard_map.99 = (bf16[128,1024]{1,0:T(8,128)(2,1)S(1)}, bf16[32,1024]{1,0:T(8,128)(2,1)S(1)}, f32[8,128]{1,0:T(8,128)S(1)}) custom-call(s32[2,2]{1,0:T(2,128)S(1)} %copy-done, bf16[128,1024]{1,0:T(8,128)(2,1)S(1)} %get-tuple-element.45.embedded_0_ref, bf16[128,3072]{1,0:T(8,128)(2,1)S(1)} %get-tuple-element.46.qkv_0_ref, ...), custom_call_target="tpu_custom_call" | custom-call | tf_op jit(solution)/shard_map/pallas_call | solution.py:499
  46.7 2.1 %collective-permute-start.5 = (bf16[32,1024]{1,0:T(8,128)(2,1)S(1)}, bf16[32,1024]{1,0:T(8,128)(2,1)S(1)}, u32[]{:S(2)}, u32[]{:S(2)}) collective-permute-start(bf16[32,1024]{1,0:T(8,128)(2,1)S(1)} %get-tuple-element.62), channel_id=1, source_target_pairs={{0,112},{16,0},{32,16},{48,32},{64,48},{80,64},{96,80},{112,96},{1... | collective-permute-start | bytes 196616 | tf_op jit(solution)/shard_map/ppermute | solution.py:504
  48.8 0.0 collective-permute-start.6
  48.8 1.2 %collective-permute-done.6 = f32[8,128]{1,0:T(8,128)S(1)} collective-permute-done((f32[8,128]{1,0:T(8,128)S(1)}, f32[8,128]{1,0:T(8,128)S(1)}, u32[]{:S(2)}, u32[]{:S(2)}) %collective-permute-start.6) | collective-permute-done | bytes 4128 | tf_op jit(solution)/shard_map/ppermute | solution.py:504
  50.0 1.0 %collective-permute-start.7 = (f32[8,128]{1,0:T(8,128)S(1)}, f32[8,128]{1,0:T(8,128)S(1)}, u32[]{:S(2)}, u32[]{:S(2)}) collective-permute-start(f32[8,128]{1,0:T(8,128)S(1)} %add.3.total_ref), channel_id=1, source_target_pairs={{0,32},{32,64},{64,96},{96,0},{1,33},{33,65},{65,97},{97,1},{2,34}... | collective-permute-start | bytes 12296 | tf_op jit(solution)/shard_map/ppermute | solution.py:504
  51.0 2.6 %collective-permute-start.8 = (f32[8,128]{1,0:T(8,128)S(1)}, f32[8,128]{1,0:T(8,128)S(1)}, u32[]{:S(2)}, u32[]{:S(2)}) collective-permute-start(f32[8,128]{1,0:T(8,128)S(1)} %add.3.total_ref), channel_id=1, source_target_pairs={{0,64},{32,96},{64,0},{96,32},{1,65},{33,97},{65,1},{97,33},{2,66}... | collective-permute-start | bytes 12296 | tf_op jit(solution)/shard_map/ppermute | solution.py:504
  53.6 1.9 %collective-permute-start.9 = (f32[8,128]{1,0:T(8,128)S(1)}, f32[8,128]{1,0:T(8,128)S(1)}, u32[]{:S(2)}, u32[]{:S(2)}) collective-permute-start(f32[8,128]{1,0:T(8,128)S(1)} %add.3.total_ref), channel_id=1, source_target_pairs={{0,96},{32,0},{64,32},{96,64},{1,97},{33,1},{65,33},{97,65},{2,98}... | collective-permute-start | bytes 12296 | tf_op jit(solution)/shard_map/ppermute | solution.py:504
  55.5 0.0 collective-permute-done.7.turned_1_ref
  55.5 0.6 collective-permute-done.8.turned_2_ref
  56.1 1.1 %collective-permute-done.9.turned_3_ref = f32[8,128]{1,0:T(8,128)S(1)} collective-permute-done((f32[8,128]{1,0:T(8,128)S(1)}, f32[8,128]{1,0:T(8,128)S(1)}, u32[]{:S(2)}, u32[]{:S(2)}) %collective-permute-start.9) | collective-permute-done | bytes 4128 | tf_op jit(solution)/shard_map/ppermute | solution.py:504
  57.2 0.0 collective-permute-done.5.next_ref
  57.3 0.2 shard_map.100
  57.5 14.8 %all_to_all.11.back_ref = bf16[16,8,1280]{2,1,0:T(8,128)(2,1)S(1)} all-to-all(bf16[16,8,1280]{2,1,0:T(8,128)(2,1)S(1)} %shard_map.100), channel_id=1, replica_groups=mesh['tm_0'=4,'tm_1'=2,'row_0'=4,'row_1'=4] {'row_0','row_1'}, dimensions={0} | all-to-all | bytes 655360 | tf_op jit(solution)/shard_map/all_to_all | solution.py:548
  72.3 0.8 %shard_map.101 = (bf16[16,4,1024]{2,1,0:T(4,128)(2,1)}, f32[8,128]{1,0:T(8,128)}) custom-call(bf16[16,8,1280]{2,1,0:T(8,128)(2,1)S(1)} %all_to_all.11.back_ref), custom_call_target="tpu_custom_call" | custom-call | tf_op jit(solution)/shard_map/pallas_call | solution.py:552
  (1 shorter events, 0.0 us)
Async XLA Ops:
  17.6 18.4 %collective-permute-start = (bf16[128,1152]{1,0:T(8,128)(2,1)S(1)}, bf16[128,1152]{1,0:T(8,128)(2,1)S(1)}, u32[]{:S(2)}, u32[]{:S(2)}) collective-permute-start(bf16[128,1152]{1,0:T(8,128)(2,1)S(1)} %bitcast.8), channel_id=1, source_target_pairs={{0,16},{16,32},{32,48},{48,64},{64,80},{80,96},{96,112},{112,0},{1... | collective-permute-start | bytes 884744 | tf_op jit(solution)/shard_map/ppermute | solution.py:504
  19.6 20.5 %collective-permute-start.1 = (bf16[3,2,16,1536]{3,2,1,0:T(8,128)(2,1)S(1)}, bf16[3,2,16,1536]{3,2,1,0:T(8,128)(2,1)S(1)}, u32[]{:S(2)}, u32[]{:S(2)}) collective-permute-start(bf16[3,2,16,1536]{3,2,1,0:T(8,128)(2,1)S(1)} %get-tuple-element.58), channel_id=1, source_target_pairs={{0,15},{1,0},{2,1},{3,2},{4,3},{5,4},{6,5},{7,6},{8,7},{9,8},{10,9... | collective-permute-start | bytes 884744 | tf_op jit(solution)/shard_map/ppermute | solution.py:504
  20.9 9.7 %collective-permute-start.2 = (bf16[1,2,16,1536]{3,2,1,0:T(8,128)(2,1)S(1)}, bf16[1,2,16,1536]{3,2,1,0:T(8,128)(2,1)S(1)}, u32[]{:S(2)}, u32[]{:S(2)}) collective-permute-start(bf16[1,2,16,1536]{3,2,1,0:T(8,128)(2,1)S(1)} %get-tuple-element.59), channel_id=1, source_target_pairs={{0,15},{1,0},{2,1},{3,2},{4,3},{5,4},{6,5},{7,6},{8,7},{9,8},{10,9... | collective-permute-start | bytes 294920 | tf_op jit(solution)/shard_map/ppermute | solution.py:504
  21.7 18.3 %collective-permute-start.3 = (bf16[1,4,16,1536]{3,2,1,0:T(8,128)(2,1)S(1)}, bf16[1,4,16,1536]{3,2,1,0:T(8,128)(2,1)S(1)}, u32[]{:S(2)}, u32[]{:S(2)}) collective-permute-start(bf16[1,4,16,1536]{3,2,1,0:T(8,128)(2,1)S(1)} %get-tuple-element.60), channel_id=1, source_target_pairs={{0,16},{16,32},{32,48},{48,64},{64,80},{80,96},{96,112},{112,0},{1... | collective-permute-start | bytes 589832 | tf_op jit(solution)/shard_map/ppermute | solution.py:504
  30.6 9.4 %collective-permute-start.4 = (bf16[1,2,16,1536]{3,2,1,0:T(8,128)(2,1)S(1)}, bf16[1,2,16,1536]{3,2,1,0:T(8,128)(2,1)S(1)}, u32[]{:S(2)}, u32[]{:S(2)}) collective-permute-start(bf16[1,2,16,1536]{3,2,1,0:T(8,128)(2,1)S(1)} %collective-permute-done.2.last_row_target), channel_id=1, source_target_pairs={{0,16},{16,32},{32,48},{48,64},{64,80},{80,96},{96,112},{112,0},{1... | collective-permute-start | bytes 294920 | tf_op jit(solution)/shard_map/ppermute | solution.py:504
  36.0 4.0 %copy-start = (s32[2,2]{1,0:T(2,128)S(1)}, s32[2,2]{1,0:T(2,128)}, u32[]{:S(2)}) copy-start(s32[2,2]{1,0:T(2,128)} %shift_ref.1) | copy-start | bytes 52
  46.7 10.6 %collective-permute-start.5 = (bf16[32,1024]{1,0:T(8,128)(2,1)S(1)}, bf16[32,1024]{1,0:T(8,128)(2,1)S(1)}, u32[]{:S(2)}, u32[]{:S(2)}) collective-permute-start(bf16[32,1024]{1,0:T(8,128)(2,1)S(1)} %get-tuple-element.62), channel_id=1, source_target_pairs={{0,112},{16,0},{32,16},{48,32},{64,48},{80,64},{96,80},{112,96},{1... | collective-permute-start | bytes 196616 | tf_op jit(solution)/shard_map/ppermute | solution.py:504
  48.8 1.2 %collective-permute-start.6 = (f32[8,128]{1,0:T(8,128)S(1)}, f32[8,128]{1,0:T(8,128)S(1)}, u32[]{:S(2)}, u32[]{:S(2)}) collective-permute-start(f32[8,128]{1,0:T(8,128)S(1)} %get-tuple-element.63), channel_id=1, source_target_pairs={{0,16},{16,0},{1,17},{17,1},{2,18},{18,2},{3,19},{19,3},{4,20},{20... | collective-permute-start | bytes 12296 | tf_op jit(solution)/shard_map/ppermute | solution.py:504
  50.0 5.6 %collective-permute-start.7 = (f32[8,128]{1,0:T(8,128)S(1)}, f32[8,128]{1,0:T(8,128)S(1)}, u32[]{:S(2)}, u32[]{:S(2)}) collective-permute-start(f32[8,128]{1,0:T(8,128)S(1)} %add.3.total_ref), channel_id=1, source_target_pairs={{0,32},{32,64},{64,96},{96,0},{1,33},{33,65},{65,97},{97,1},{2,34}... | collective-permute-start | bytes 12296 | tf_op jit(solution)/shard_map/ppermute | solution.py:504
  51.0 5.1 %collective-permute-start.8 = (f32[8,128]{1,0:T(8,128)S(1)}, f32[8,128]{1,0:T(8,128)S(1)}, u32[]{:S(2)}, u32[]{:S(2)}) collective-permute-start(f32[8,128]{1,0:T(8,128)S(1)} %add.3.total_ref), channel_id=1, source_target_pairs={{0,64},{32,96},{64,0},{96,32},{1,65},{33,97},{65,1},{97,33},{2,66}... | collective-permute-start | bytes 12296 | tf_op jit(solution)/shard_map/ppermute | solution.py:504
  53.6 3.6 %collective-permute-start.9 = (f32[8,128]{1,0:T(8,128)S(1)}, f32[8,128]{1,0:T(8,128)S(1)}, u32[]{:S(2)}, u32[]{:S(2)}) collective-permute-start(f32[8,128]{1,0:T(8,128)S(1)} %add.3.total_ref), channel_id=1, source_target_pairs={{0,96},{32,0},{64,32},{96,64},{1,97},{33,1},{65,33},{97,65},{2,98}... | collective-permute-start | bytes 12296 | tf_op jit(solution)/shard_map/ppermute | solution.py:504
